TPU v7x, 8 devices: a whole 2x2x1 slice. The times are simulated.
8 devices in a mesh: stage: 1 (over z), fsdp: 2 (over y), tp: 4 (over x, core).
Axes of the slice: x: 2, y: 2, z: 1, core: 2. Of those that a mesh axis runs over, the one named last changes fastest.
Arguments:
- weight: float32 [1, 11008, 4096], P('stage', 'fsdp', 'tp')
- momentum: float32 [1, 11008, 4096], P('stage', 'fsdp', 'tp')
- gradient: bfloat16 [1, 11008, 4096], P('stage', 'fsdp', 'tp')
- learn_rate: float32 [], replicated
- mom_coef: float32 [], replicated
- weight_decay: float32 [], replicated
Outputs:
- output 1: float32 [1, 11008, 4096], P('stage', 'fsdp', 'tp')
- output 2: float32 [1, 11008, 4096], P('stage', 'fsdp', 'tp')
All inputs are finite; a program needn't handle non-finite values.
Results may differ from a plain program's by a relative error of at most 0.00931572.
Values are sent between devices in bfloat16 or wider.
A program may use at most 1 GiB of HBM per device.

v0:
```python
import jax
import jax.numpy as jnp
from jax import lax
from jax.sharding import PartitionSpec as P
import math

NS_STEPS = 5
COEF_A = 3.4445
COEF_B = -4.7750
COEF_C = 2.0315
NORM_EPS = 1e-7


def solution(mesh):
    fsdp_size = mesh.shape['fsdp']
    mat_spec = P('stage', 'fsdp', 'tp')
    scalar_spec = P()

    def local_step(weight, momentum, gradient, learn_rate, mom_coef, weight_decay):
        row_dim = weight.shape[1] * fsdp_size
        grad_full = gradient.astype(jnp.float32)
        mom_new = mom_coef * momentum + grad_full
        nesterov = grad_full + mom_coef * mom_new
        sq_sum = lax.psum(jnp.sum(nesterov * nesterov, axis=(1, 2)), ('fsdp', 'tp'))
        norm_val = jnp.sqrt(sq_sum)[:, None, None]
        x_iter = (nesterov / (norm_val + NORM_EPS)).astype(jnp.bfloat16)
        for step_idx in range(NS_STEPS):
            x_rows = lax.all_gather(x_iter, 'tp', axis=2, tiled=True)
            gram_part = jnp.einsum('erc,erd->ecd', x_iter, x_rows, preferred_element_type=jnp.float32)
            gram_blk = lax.psum_scatter(gram_part, 'fsdp', scatter_dimension=2, tiled=True).astype(jnp.bfloat16)
            gram_cols = lax.all_gather(gram_blk, 'tp', axis=1, tiled=True)
            gram_rows = lax.all_gather(gram_blk, 'fsdp', axis=2, tiled=True)
            gram_sq = jnp.einsum('eab,ebc->eac', gram_rows, gram_cols, preferred_element_type=jnp.float32).astype(jnp.bfloat16)
            poly_blk = (COEF_B * gram_blk.astype(jnp.float32) + COEF_C * gram_sq.astype(jnp.float32)).astype(jnp.bfloat16)
            poly_rows = lax.all_gather(poly_blk, 'fsdp', axis=2, tiled=True)
            update = jnp.einsum('erk,eck->erc', x_rows, poly_rows, preferred_element_type=jnp.float32)
            x_iter = (COEF_A * x_iter.astype(jnp.float32) + update).astype(jnp.bfloat16)
        step_scale = learn_rate * 0.2 * math.sqrt(row_dim)
        new_weight = (1.0 - learn_rate * weight_decay) * weight - step_scale * x_iter.astype(jnp.float32)
        return new_weight, mom_new

    return jax.shard_map(local_step, mesh=mesh, in_specs=(mat_spec,) * 3 + (scalar_spec,) * 3, out_specs=(mat_spec, mat_spec), check_vma=False)
```

profile of v0, /device:TPU:0, one launch (start us, length us, event | category | flops | bytes accessed | tf_op | source)
XLA Modules:
  0.0 4614.5 jit_solution(3887331519422033303)
XLA Ops:
  71.2 266.0 %all-gather.21.cloned.1.call-done = bf16[1,5504,4096]{2,1,0:T(8,128)(2,1)} async-done(((bf16[1,5504,1024]{2,1,0:T(8,128)(2,1)}), bf16[1,5504,4096]{2,1,0:T(8,128)(2,1)}) %all-gather.21.cloned.1.call-update) | async-done | bytes 45088784 | tf_op jit(solution)/shard_map/all_gather | solution.py:28
  337.2 58.3 %fusion.52 = f32[1,1024,4096]{2,1,0:T(8,128)} fusion(bf16[1,5504,4096]{2,1,0:T(8,128)(2,1)} %all-gather.21.cloned.1.call-done, bf16[1,5504,1024]{2,1,0:T(8,128)(2,1)} %divide_convert_fusion), kind=kOutput, calls=%fused_computation.50 | convolution fusion | flops 46170898432 | bytes 73138176 | tf_op jit(solution)/shard_map/erc,erd->ecd/dot_general | solution.py:29
  395.6 186.4 %reduce-scatter.6.cloned.1.call-done = f32[1,1024,2048]{2,1,0:T(8,128)} async-done(((f32[1,1024,4096]{2,1,0:T(8,128)}), f32[1,1024,2048]{2,1,0:T(8,128)}) %reduce-scatter.6.cloned.1.call-update) | async-done | bytes 8388624 | tf_op jit(solution)/shard_map/reduce_scatter | solution.py:30
  588.8 101.6 %all-gather.23.cloned.1.call-done = bf16[1,1024,4096]{2,1,0:T(8,128)(2,1)} async-done(((bf16[1,1024,2048]{2,1,0:T(8,128)(2,1)}), bf16[1,1024,4096]{2,1,0:T(8,128)(2,1)}) %all-gather.23.cloned.1.call-update) | async-done | bytes 8388624 | tf_op jit(solution)/shard_map/all_gather | solution.py:32
  690.5 106.2 %all-gather.25.cloned.1.call-done = bf16[1,4096,2048]{2,1,0:T(8,128)(2,1)} async-done(((bf16[1,1024,2048]{2,1,0:T(8,128)(2,1)}), bf16[1,4096,2048]{2,1,0:T(8,128)(2,1)}) %all-gather.25.cloned.1.call-update) | async-done | bytes 16777232 | tf_op jit(solution)/shard_map/all_gather | solution.py:31
  820.9 102.4 %all-gather.27.cloned.1.call-done = bf16[1,1024,4096]{2,1,0:T(8,128)(2,1)} async-done(((bf16[1,1024,2048]{2,1,0:T(8,128)(2,1)}), bf16[1,1024,4096]{2,1,0:T(8,128)(2,1)}) %all-gather.27.cloned.1.call-update) | async-done | bytes 8388624 | tf_op jit(solution)/shard_map/all_gather | solution.py:35
  923.3 54.8 %fusion.24 = bf16[1,5504,1024]{2,1,0:T(8,128)(2,1)} fusion(bf16[1,5504,1024]{2,1,0:T(8,128)(2,1)} %divide_convert_fusion, bf16[1,5504,4096]{2,1,0:T(8,128)(2,1)} %all-gather.21.cloned.1.call-done, bf16[1,1024,4096]{2,1,0:T(8,128)(2,1)} %all-gather.27.cloned.1.call-done), kind=kOutput, calls=%fused_computation.31 | convolution fusion | flops 46193442816 | bytes 76021760 | tf_op jit(solution)/shard_map/erk,eck->erc/dot_general | solution.py:36
  978.4 265.3 %all-gather.29.cloned.1.call-done = bf16[1,5504,4096]{2,1,0:T(8,128)(2,1)} async-done(((bf16[1,5504,1024]{2,1,0:T(8,128)(2,1)}), bf16[1,5504,4096]{2,1,0:T(8,128)(2,1)}) %all-gather.29.cloned.1.call-update) | async-done | bytes 45088784 | tf_op jit(solution)/shard_map/all_gather | solution.py:28
  1243.7 58.3 %fusion.57 = f32[1,1024,4096]{2,1,0:T(8,128)} fusion(bf16[1,5504,4096]{2,1,0:T(8,128)(2,1)} %all-gather.29.cloned.1.call-done, bf16[1,5504,1024]{2,1,0:T(8,128)(2,1)} %fusion.24), kind=kOutput, calls=%fused_computation.51 | convolution fusion | flops 46170898432 | bytes 73138176 | tf_op jit(solution)/shard_map/erc,erd->ecd/dot_general | solution.py:29
  1302.1 186.4 %reduce-scatter.8.cloned.1.call-done = f32[1,1024,2048]{2,1,0:T(8,128)} async-done(((f32[1,1024,4096]{2,1,0:T(8,128)}), f32[1,1024,2048]{2,1,0:T(8,128)}) %reduce-scatter.8.cloned.1.call-update) | async-done | bytes 8388624 | tf_op jit(solution)/shard_map/reduce_scatter | solution.py:30
  1495.8 101.2 %all-gather.31.cloned.1.call-done = bf16[1,1024,4096]{2,1,0:T(8,128)(2,1)} async-done(((bf16[1,1024,2048]{2,1,0:T(8,128)(2,1)}), bf16[1,1024,4096]{2,1,0:T(8,128)(2,1)}) %all-gather.31.cloned.1.call-update) | async-done | bytes 8388624 | tf_op jit(solution)/shard_map/all_gather | solution.py:32
  1597.0 106.3 %all-gather.33.cloned.1.call-done = bf16[1,4096,2048]{2,1,0:T(8,128)(2,1)} async-done(((bf16[1,1024,2048]{2,1,0:T(8,128)(2,1)}), bf16[1,4096,2048]{2,1,0:T(8,128)(2,1)}) %all-gather.33.cloned.1.call-update) | async-done | bytes 16777232 | tf_op jit(solution)/shard_map/all_gather | solution.py:31
  1727.6 102.4 %all-gather.35.cloned.1.call-done = bf16[1,1024,4096]{2,1,0:T(8,128)(2,1)} async-done(((bf16[1,1024,2048]{2,1,0:T(8,128)(2,1)}), bf16[1,1024,4096]{2,1,0:T(8,128)(2,1)}) %all-gather.35.cloned.1.call-update) | async-done | bytes 8388624 | tf_op jit(solution)/shard_map/all_gather | solution.py:35
  1885.1 265.3 %all-gather.37.cloned.1.call-done = bf16[1,5504,4096]{2,1,0:T(8,128)(2,1)} async-done(((bf16[1,5504,1024]{2,1,0:T(8,128)(2,1)}), bf16[1,5504,4096]{2,1,0:T(8,128)(2,1)}) %all-gather.37.cloned.1.call-update) | async-done | bytes 45088784 | tf_op jit(solution)/shard_map/all_gather | solution.py:28
  2150.4 58.3 %fusion.62 = f32[1,1024,4096]{2,1,0:T(8,128)} fusion(bf16[1,5504,4096]{2,1,0:T(8,128)(2,1)} %all-gather.37.cloned.1.call-done, bf16[1,5504,1024]{2,1,0:T(8,128)(2,1)} %fusion.23), kind=kOutput, calls=%fused_computation.52 | convolution fusion | flops 46170898432 | bytes 73138176 | tf_op jit(solution)/shard_map/erc,erd->ecd/dot_general | solution.py:29
  2208.8 186.4 %reduce-scatter.10.cloned.1.call-done = f32[1,1024,2048]{2,1,0:T(8,128)} async-done(((f32[1,1024,4096]{2,1,0:T(8,128)}), f32[1,1024,2048]{2,1,0:T(8,128)}) %reduce-scatter.10.cloned.1.call-update) | async-done | bytes 8388624 | tf_op jit(solution)/shard_map/reduce_scatter | solution.py:30
  2402.2 101.6 %all-gather.39.cloned.1.call-done = bf16[1,1024,4096]{2,1,0:T(8,128)(2,1)} async-done(((bf16[1,1024,2048]{2,1,0:T(8,128)(2,1)}), bf16[1,1024,4096]{2,1,0:T(8,128)(2,1)}) %all-gather.39.cloned.1.call-update) | async-done | bytes 8388624 | tf_op jit(solution)/shard_map/all_gather | solution.py:32
  2503.8 106.2 %all-gather.41.cloned.1.call-done = bf16[1,4096,2048]{2,1,0:T(8,128)(2,1)} async-done(((bf16[1,1024,2048]{2,1,0:T(8,128)(2,1)}), bf16[1,4096,2048]{2,1,0:T(8,128)(2,1)}) %all-gather.41.cloned.1.call-update) | async-done | bytes 16777232 | tf_op jit(solution)/shard_map/all_gather | solution.py:31
  2634.2 102.4 %all-gather.43.cloned.1.call-done = bf16[1,1024,4096]{2,1,0:T(8,128)(2,1)} async-done(((bf16[1,1024,2048]{2,1,0:T(8,128)(2,1)}), bf16[1,1024,4096]{2,1,0:T(8,128)(2,1)}) %all-gather.43.cloned.1.call-update) | async-done | bytes 8388624 | tf_op jit(solution)/shard_map/all_gather | solution.py:35
  2791.9 265.1 %all-gather.45.cloned.1.call-done = bf16[1,5504,4096]{2,1,0:T(8,128)(2,1)} async-done(((bf16[1,5504,1024]{2,1,0:T(8,128)(2,1)}), bf16[1,5504,4096]{2,1,0:T(8,128)(2,1)}) %all-gather.45.cloned.1.call-update) | async-done | bytes 45088784 | tf_op jit(solution)/shard_map/all_gather | solution.py:28
  3057.0 58.3 %fusion.67 = f32[1,1024,4096]{2,1,0:T(8,128)} fusion(bf16[1,5504,4096]{2,1,0:T(8,128)(2,1)} %all-gather.45.cloned.1.call-done, bf16[1,5504,1024]{2,1,0:T(8,128)(2,1)} %fusion.22), kind=kOutput, calls=%fused_computation.53 | convolution fusion | flops 46170898432 | bytes 73138176 | tf_op jit(solution)/shard_map/erc,erd->ecd/dot_general | solution.py:29
  3115.4 186.4 %reduce-scatter.12.cloned.1.call-done = f32[1,1024,2048]{2,1,0:T(8,128)} async-done(((f32[1,1024,4096]{2,1,0:T(8,128)}), f32[1,1024,2048]{2,1,0:T(8,128)}) %reduce-scatter.12.cloned.1.call-update) | async-done | bytes 8388624 | tf_op jit(solution)/shard_map/reduce_scatter | solution.py:30
  3308.9 101.5 %all-gather.47.cloned.1.call-done = bf16[1,1024,4096]{2,1,0:T(8,128)(2,1)} async-done(((bf16[1,1024,2048]{2,1,0:T(8,128)(2,1)}), bf16[1,1024,4096]{2,1,0:T(8,128)(2,1)}) %all-gather.47.cloned.1.call-update) | async-done | bytes 8388624 | tf_op jit(solution)/shard_map/all_gather | solution.py:32
  3410.3 106.3 %all-gather.49.cloned.1.call-done = bf16[1,4096,2048]{2,1,0:T(8,128)(2,1)} async-done(((bf16[1,1024,2048]{2,1,0:T(8,128)(2,1)}), bf16[1,4096,2048]{2,1,0:T(8,128)(2,1)}) %all-gather.49.cloned.1.call-update) | async-done | bytes 16777232 | tf_op jit(solution)/shard_map/all_gather | solution.py:31
  3540.9 102.4 %all-gather.51.cloned.1.call-done = bf16[1,1024,4096]{2,1,0:T(8,128)(2,1)} async-done(((bf16[1,1024,2048]{2,1,0:T(8,128)(2,1)}), bf16[1,1024,4096]{2,1,0:T(8,128)(2,1)}) %all-gather.51.cloned.1.call-update) | async-done | bytes 8388624 | tf_op jit(solution)/shard_map/all_gather | solution.py:35
  3698.4 265.3 %all-gather.53.cloned.1.call-done = bf16[1,5504,4096]{2,1,0:T(8,128)(2,1)} async-done(((bf16[1,5504,1024]{2,1,0:T(8,128)(2,1)}), bf16[1,5504,4096]{2,1,0:T(8,128)(2,1)}) %all-gather.53.cloned.1.call-update) | async-done | bytes 45088784 | tf_op jit(solution)/shard_map/all_gather | solution.py:28
  3963.7 58.3 %fusion.72 = f32[1,1024,4096]{2,1,0:T(8,128)} fusion(bf16[1,5504,4096]{2,1,0:T(8,128)(2,1)} %all-gather.53.cloned.1.call-done, bf16[1,5504,1024]{2,1,0:T(8,128)(2,1)} %fusion.21), kind=kOutput, calls=%fused_computation.54 | convolution fusion | flops 46170898432 | bytes 73138176 | tf_op jit(solution)/shard_map/erc,erd->ecd/dot_general | solution.py:29
  4022.1 186.4 %reduce-scatter.14.cloned.1.call-done = f32[1,1024,2048]{2,1,0:T(8,128)} async-done(((f32[1,1024,4096]{2,1,0:T(8,128)}), f32[1,1024,2048]{2,1,0:T(8,128)}) %reduce-scatter.14.cloned.1.call-update) | async-done | bytes 8388624 | tf_op jit(solution)/shard_map/reduce_scatter | solution.py:30
  4215.4 101.6 %all-gather.55.cloned.1.call-done = bf16[1,1024,4096]{2,1,0:T(8,128)(2,1)} async-done(((bf16[1,1024,2048]{2,1,0:T(8,128)(2,1)}), bf16[1,1024,4096]{2,1,0:T(8,128)(2,1)}) %all-gather.55.cloned.1.call-update) | async-done | bytes 8388624 | tf_op jit(solution)/shard_map/all_gather | solution.py:32
  4317.0 106.2 %all-gather.57.cloned.1.call-done = bf16[1,4096,2048]{2,1,0:T(8,128)(2,1)} async-done(((bf16[1,1024,2048]{2,1,0:T(8,128)(2,1)}), bf16[1,4096,2048]{2,1,0:T(8,128)(2,1)}) %all-gather.57.cloned.1.call-update) | async-done | bytes 16777232 | tf_op jit(solution)/shard_map/all_gather | solution.py:31
  4448.7 101.1 %all-gather.59.cloned.1.call-done = bf16[1,1024,4096]{2,1,0:T(8,128)(2,1)} async-done(((bf16[1,1024,2048]{2,1,0:T(8,128)(2,1)}), bf16[1,1024,4096]{2,1,0:T(8,128)(2,1)}) %all-gather.59.cloned.1.call-update) | async-done | bytes 8388624 | tf_op jit(solution)/shard_map/all_gather | solution.py:35
  4549.8 57.9 %multiply_subtract_fusion = f32[1,5504,1024]{2,1,0:T(8,128)} fusion(f32[1,5504,1024]{2,1,0:T(8,128)} %param.6, bf16[1,5504,4096]{2,1,0:T(8,128)(2,1)} %all-gather.53.cloned.1.call-done, bf16[1,5504,1024]{2,1,0:T(8,128)(2,1)} %fusion.21, f32[]{:T(128)S(6)} %mul.95, f32[]{:T(128)S(6)} %sub.6, bf16[1,1024,4096]{2,1,0:T(8,128)(2,1)} %all-gather.59.cloned.1.call-done), kind=kOutput, calls=%fused_computation.32 | convolution fusion | flops 46215987200 | bytes 109838344 | tf_op jit(solution)/shard_map/erk,eck->erc/dot_general | solution.py:36
  (66 shorter events, 384.8 us)
Async XLA Ops:
  7.2 330.0 %all-gather.21.cloned.1.call-start = ((), (), s32[]{:S(2)}) async-start(), calls=%async_computation.5 | async-start | bytes 56360960 | tf_op jit(solution)/shard_map/all_gather | solution.py:28
  70.6 511.4 %reduce-scatter.6.cloned.1.call-start = ((), (), s32[]{:S(2)}) async-start(), calls=%async_computation.6 | async-start | bytes 25165824 | tf_op jit(solution)/shard_map/reduce_scatter | solution.py:30
  395.5 295.0 %all-gather.23.cloned.1.call-start = ((), (), s32[]{:S(2)}) async-start(), calls=%async_computation.7 | async-start | bytes 12582912 | tf_op jit(solution)/shard_map/all_gather | solution.py:32
  588.0 208.6 %all-gather.25.cloned.1.call-start = ((), (), s32[]{:S(2)}) async-start(), calls=%async_computation.8 | async-start | bytes 20971520 | tf_op jit(solution)/shard_map/all_gather | solution.py:31
  588.6 334.7 %all-gather.27.cloned.1.call-start = ((), (), s32[]{:S(2)}) async-start(), calls=%async_computation.9 | async-start | bytes 12582912 | tf_op jit(solution)/shard_map/all_gather | solution.py:35
  820.9 422.8 %all-gather.29.cloned.1.call-start = ((), (), s32[]{:S(2)}) async-start(), calls=%async_computation.10 | async-start | bytes 56360960 | tf_op jit(solution)/shard_map/all_gather | solution.py:28
  978.2 510.4 %reduce-scatter.8.cloned.1.call-start = ((), (), s32[]{:S(2)}) async-start(), calls=%async_computation.11 | async-start | bytes 25165824 | tf_op jit(solution)/shard_map/reduce_scatter | solution.py:30
  1302.1 295.0 %all-gather.31.cloned.1.call-start = ((), (), s32[]{:S(2)}) async-start(), calls=%async_computation.12 | async-start | bytes 12582912 | tf_op jit(solution)/shard_map/all_gather | solution.py:32
  1494.6 208.8 %all-gather.33.cloned.1.call-start = ((), (), s32[]{:S(2)}) async-start(), calls=%async_computation.13 | async-start | bytes 20971520 | tf_op jit(solution)/shard_map/all_gather | solution.py:31
  1495.3 334.7 %all-gather.35.cloned.1.call-start = ((), (), s32[]{:S(2)}) async-start(), calls=%async_computation.14 | async-start | bytes 12582912 | tf_op jit(solution)/shard_map/all_gather | solution.py:35
  1727.6 422.9 %all-gather.37.cloned.1.call-start = ((), (), s32[]{:S(2)}) async-start(), calls=%async_computation.15 | async-start | bytes 56360960 | tf_op jit(solution)/shard_map/all_gather | solution.py:28
  1884.9 510.4 %reduce-scatter.10.cloned.1.call-start = ((), (), s32[]{:S(2)}) async-start(), calls=%async_computation.16 | async-start | bytes 25165824 | tf_op jit(solution)/shard_map/reduce_scatter | solution.py:30
  2208.8 295.0 %all-gather.39.cloned.1.call-start = ((), (), s32[]{:S(2)}) async-start(), calls=%async_computation.17 | async-start | bytes 12582912 | tf_op jit(solution)/shard_map/all_gather | solution.py:32
  2401.3 208.6 %all-gather.41.cloned.1.call-start = ((), (), s32[]{:S(2)}) async-start(), calls=%async_computation.18 | async-start | bytes 20971520 | tf_op jit(solution)/shard_map/all_gather | solution.py:31
  2401.9 334.7 %all-gather.43.cloned.1.call-start = ((), (), s32[]{:S(2)}) async-start(), calls=%async_computation.19 | async-start | bytes 12582912 | tf_op jit(solution)/shard_map/all_gather | solution.py:35
  2634.1 422.9 %all-gather.45.cloned.1.call-start = ((), (), s32[]{:S(2)}) async-start(), calls=%async_computation.20 | async-start | bytes 56360960 | tf_op jit(solution)/shard_map/all_gather | solution.py:28
  2791.4 510.4 %reduce-scatter.12.cloned.1.call-start = ((), (), s32[]{:S(2)}) async-start(), calls=%async_computation.21 | async-start | bytes 25165824 | tf_op jit(solution)/shard_map/reduce_scatter | solution.py:30
  3115.3 295.0 %all-gather.47.cloned.1.call-start = ((), (), s32[]{:S(2)}) async-start(), calls=%async_computation.22 | async-start | bytes 12582912 | tf_op jit(solution)/shard_map/all_gather | solution.py:32
  3307.9 208.7 %all-gather.49.cloned.1.call-start = ((), (), s32[]{:S(2)}) async-start(), calls=%async_computation.23 | async-start | bytes 20971520 | tf_op jit(solution)/shard_map/all_gather | solution.py:31
  3308.6 334.6 %all-gather.51.cloned.1.call-start = ((), (), s32[]{:S(2)}) async-start(), calls=%async_computation.24 | async-start | bytes 12582912 | tf_op jit(solution)/shard_map/all_gather | solution.py:35
  3540.8 422.8 %all-gather.53.cloned.1.call-start = ((), (), s32[]{:S(2)}) async-start(), calls=%async_computation.25 | async-start | bytes 56360960 | tf_op jit(solution)/shard_map/all_gather | solution.py:28
  3698.1 510.4 %reduce-scatter.14.cloned.1.call-start = ((), (), s32[]{:S(2)}) async-start(), calls=%async_computation.26 | async-start | bytes 25165824 | tf_op jit(solution)/shard_map/reduce_scatter | solution.py:30
  4022.0 295.0 %all-gather.55.cloned.1.call-start = ((), (), s32[]{:S(2)}) async-start(), calls=%async_computation.27 | async-start | bytes 12582912 | tf_op jit(solution)/shard_map/all_gather | solution.py:32
  4214.6 208.6 %all-gather.57.cloned.1.call-start = ((), (), s32[]{:S(2)}) async-start(), calls=%async_computation.28 | async-start | bytes 20971520 | tf_op jit(solution)/shard_map/all_gather | solution.py:31
  4215.2 334.7 %all-gather.59.cloned.1.call-start = ((), (), s32[]{:S(2)}) async-start(), calls=%async_computation.29 | async-start | bytes 12582912 | tf_op jit(solution)/shard_map/all_gather | solution.py:35
Sparse Core Ops, SparseCore 0:
  70.7 266.3 all-gather.20
  395.6 186.2 reduce-scatter.5
  588.2 102.2 all-gather.22
  692.4 104.1 all-gather.24
  821.0 102.2 all-gather.26
  978.3 265.3 all-gather.28
  1302.2 186.2 reduce-scatter.7
  1494.7 102.2 all-gather.30
  1599.1 104.1 all-gather.32
  1727.7 102.2 all-gather.34
  1885.0 265.3 all-gather.36
  2208.9 186.2 reduce-scatter.9
  2401.4 102.2 all-gather.38
  2505.7 104.1 all-gather.40
  2634.3 102.2 all-gather.42
  2791.6 265.3 all-gather.44
  3115.5 186.2 reduce-scatter.11
  3308.0 102.2 all-gather.46
  3412.4 104.1 all-gather.48
  3541.0 102.2 all-gather.50
  3698.2 265.3 all-gather.52
  4022.2 186.2 reduce-scatter.13
  4214.7 102.2 all-gather.54
  4319.0 104.1 all-gather.56
  4447.5 102.2 all-gather.58
where the time goes:
time: 4620 us; the launch traced here: 4610 us
  waiting for transfers between devices  3810 us (82%)
  matrix products  690 us (15%)
  other arithmetic  67 us (1%)
    all_gather x5, waiting for transfers between devices, local_step(): x_rows = lax.all_gather(x_iter, 'tp', axis=2, tiled=True)  1330 us
    reduce_scatter x5, waiting for transfers between devices, local_step(): lax.psum_scatter(gram_part, 'fsdp', scatter_dimension=2, tiled=True)  932 us
    all_gather x5, waiting for transfers between devices, local_step(): gram_cols = lax.all_gather(gram_blk, 'tp', axis=1, tiled=True)  531 us
    all_gather x5, waiting for transfers between devices, local_step(): poly_rows = lax.all_gather(poly_blk, 'fsdp', axis=2, tiled=True)  511 us
    all_gather x5, waiting for transfers between devices, local_step(): gram_rows = lax.all_gather(gram_blk, 'fsdp', axis=2, tiled=True)  507 us
    dot_general x5, matrix products, local_step(): jnp.einsum('erc,erd->ecd', x_iter, x_rows, preferred_element_type=jnp.flo...  292 us
    dot_general x5, matrix products, local_step(): jnp.einsum('erk,eck->erc', x_rows, poly_rows, preferred_element_type=jnp....  277 us
    dot_general x5, matrix products, local_step(): jnp.einsum('eab,ebc->eac', gram_rows, gram_cols, preferred_element_type=j...  121 us
  transfers between devices with their start and end apart: 25, of which 25 were waited for; matrix products, arithmetic and copies ran while one was open for 0% of the time, Pallas kernels for 0%

commit v1 on v0

v1 whole, which is shorter than its diff:
```python
import functools
import math

import jax
import jax.numpy as jnp
from jax import lax
from jax.experimental import pallas as pl
from jax.experimental.pallas import tpu as pltpu
from jax.sharding import PartitionSpec as P


NS_STEPS = 5
COEF_A = 3.4445
COEF_B = -4.7750
COEF_C = 2.0315
NORM_EPS = 1e-7


BS = 512
VMEM_LIMIT = 58 * 1024 * 1024
BF16, F32 = jnp.bfloat16, jnp.float32
CORE, ZERO, XPOS, YPOS, KEEP, SEND, MINE, SEL = 8, 9, 10, 11, 12, 13, 14, 16


def call(kernel, grid, in_specs, out_specs, out_shape, idx, args, flops, nbytes, scratch=(), aliases=None):
    return pl.pallas_call(
        kernel,
        grid_spec=pltpu.PrefetchScalarGridSpec(
            num_scalar_prefetch=1, grid=grid, in_specs=in_specs, out_specs=out_specs, scratch_shapes=scratch
        ),
        out_shape=out_shape,
        input_output_aliases=aliases or {},
        compiler_params=pltpu.CompilerParams(
            vmem_limit_bytes=VMEM_LIMIT, dimension_semantics=('arbitrary',) * len(grid)
        ),
        cost_estimate=pl.CostEstimate(flops=flops, bytes_accessed=nbytes, transcendentals=0),
    )(idx, *args)


class Order:
    def __init__(self, idx):
        self.idx = idx

    def after(self, *arrays):
        self.idx = lax.optimization_barrier((self.idx,) + arrays)[0]


def start_kernel(mom_ref, grad_ref, scal_ref, out_ref):
    grad = grad_ref[...].astype(F32)
    nesterov = grad + scal_ref[0] * (scal_ref[0] * mom_ref[...] + grad)
    out_ref[...] = (nesterov / scal_ref[1]).astype(BF16).T


def start_x(momentum, gradient, scalars):
    rows, cols = momentum.shape
    spec = pl.BlockSpec((BS, cols), lambda i: (i, 0))
    return pl.pallas_call(
        start_kernel,
        name='start',
        grid=(pl.cdiv(rows, BS),),
        in_specs=[spec, spec, pl.BlockSpec(memory_space=pltpu.SMEM)],
        out_specs=pl.BlockSpec((cols, BS), lambda i: (0, i)),
        out_shape=jax.ShapeDtypeStruct((cols, rows), BF16),
        compiler_params=pltpu.CompilerParams(vmem_limit_bytes=VMEM_LIMIT, dimension_semantics=('arbitrary',)),
        cost_estimate=pl.CostEstimate(flops=rows * cols * 64, bytes_accessed=rows * cols * 8, transcendentals=0),
    )(momentum, gradient, scalars)


def gram_kernel(depth, tile, idx_ref, rows_ref, *refs):
    keep_ref, send_ref = refs[-2:]
    step = pl.program_id(0)
    n_steps = pl.cdiv(depth, tile)
    rest = depth - (n_steps - 1) * tile

    def product(width):
        lhs = jnp.concatenate([ref[0, :, :width] for ref in refs[:-2]], axis=0)
        acc = jnp.dot(lhs, rows_ref[0, :, :width].T, preferred_element_type=F32)
        half = acc.shape[0] // 2
        return acc[:half].reshape(keep_ref.shape), acc[half:].reshape(send_ref.shape)

    @pl.when(step == 0)
    def _():
        keep_ref[...], send_ref[...] = product(tile)

    @pl.when((step > 0) & (step < n_steps - 1))
    def _():
        keep, send = product(tile)
        keep_ref[...] += keep
        send_ref[...] += send

    @pl.when(step == n_steps - 1)
    def _():
        keep, send = product(rest)
        keep_ref[...] += keep
        send_ref[...] += send


def gram_unit(idx, pieces, q, p_lo, p_hi):
    num = 2 * (p_hi - p_lo)
    rows_arr, rows_at = pieces[2 * q]
    depth = rows_arr.shape[-1]
    tile = pl.cdiv(depth, 4 * 128) * 128
    in_specs = [pl.BlockSpec((1, BS, tile), lambda k, s: (s[rows_at], 0, k))]
    args = [rows_arr]
    for part in (KEEP, SEND):
        for arr, at in pieces[2 * p_lo:2 * p_hi]:
            in_specs.append(pl.BlockSpec((1, BS // 4, tile), lambda k, s, at=at, part=part: (s[at], s[part], k)))
            args.append(arr)
    out = jax.ShapeDtypeStruct((num, BS // 4, BS), F32)
    out_spec = pl.BlockSpec((num, BS // 4, BS), lambda k, s: (0, 0, 0))
    return call(
        functools.partial(gram_kernel, depth, tile), (pl.cdiv(depth, tile),),
        in_specs, (out_spec, out_spec), (out, out), idx, args,
        2 * num * (BS // 2) * BS * depth, (num + 2) * BS * depth,
    )


def square_kernel(idx_ref, rows_ref, cols_ref, own_ref, out_ref):
    acc = jnp.dot(rows_ref[...], cols_ref[...], preferred_element_type=F32)
    sq = acc.astype(BF16).astype(F32)
    out_ref[...] = (COEF_B * own_ref[...].astype(F32) + COEF_C * sq).astype(BF16)


def poly_rows(idx, gram, row_at):
    dim = gram.shape[0]
    num = dim // BS
    in_specs = [
        pl.BlockSpec((BS, dim), lambda i, s: (s[row_at], 0)),
        pl.BlockSpec((dim, BS), lambda i, s: (0, i)),
        pl.BlockSpec((BS, BS), lambda i, s: (s[row_at], i)),
    ]
    out_spec = pl.BlockSpec((BS, BS), lambda i, s: (0, jnp.bitwise_xor(i, s[CORE])))
    return call(
        square_kernel, (num,), in_specs, out_spec,
        jax.ShapeDtypeStruct((BS, dim), BF16), idx, [gram, gram, gram], 2 * BS * dim * dim, dim * dim * 2,
    )


def mix(b_ref, refs):
    acc = jnp.dot(b_ref[:, :BS], refs[0][0], preferred_element_type=F32)
    for pos in range(1, len(refs)):
        acc += jnp.dot(b_ref[:, pos * BS:(pos + 1) * BS], refs[pos][0], preferred_element_type=F32)
    return acc


def update_kernel(sel, idx_ref, b_ref, *refs):
    out_ref = refs[-1]
    acc = mix(b_ref, refs[:-1])
    out_ref[0] = (COEF_A * refs[sel][0].astype(F32) + acc).astype(BF16)


def piece_specs(pieces, tile):
    specs = [pl.BlockSpec((1, BS, tile), lambda i, s, at=at: (s[at], 0, i)) for _, at in pieces]
    return specs, [arr for arr, _ in pieces]


def update_chunk(idx, poly, pieces, q):
    num = len(pieces)
    depth = pieces[0][0].shape[-1]
    tile = BS
    specs, args = piece_specs(pieces, tile)
    return call(
        functools.partial(update_kernel, 2 * q), (pl.cdiv(depth, tile),),
        [pl.BlockSpec(poly.shape, lambda i, s: (0, 0))] + specs, pl.BlockSpec((1, BS, tile), lambda i, s: (0, 0, i)),
        jax.ShapeDtypeStruct((1, BS, depth), BF16), idx, [poly] + args,
        2 * BS * BS * num * depth, num * BS * depth * 2,
    )


def finish_kernel(half, num, idx_ref, scal_ref, b_ref, w_ref, *refs):
    old_ref = refs[-1]
    out_ref = refs[num]
    acc = mix(b_ref, refs[:num])
    for pos in range(num):
        @pl.when(idx_ref[SEL + half] == pos)
        def _(pos=pos):
            old_ref[...] = refs[pos][0]
    x_last = (COEF_A * old_ref[...].astype(F32) + acc).astype(BF16).T
    out_ref[...] = scal_ref[0] * w_ref[...] - scal_ref[1] * x_last.astype(F32)


def finish(idx, scalars, poly, weight, pieces, half, before):
    num = len(pieces)
    rows = weight.shape[0]
    tile = BS
    specs, args = piece_specs(pieces, tile)
    w_spec = pl.BlockSpec((tile, BS), lambda i, s: (i, half))
    in_specs = [pl.BlockSpec(memory_space=pltpu.SMEM), pl.BlockSpec(poly.shape, lambda i, s: (0, 0)), w_spec] + specs
    args = [scalars, poly, weight] + args
    kernel = functools.partial(finish_kernel, half, num)
    aliases = None
    if before is not None:
        in_specs.append(pl.BlockSpec(memory_space=pl.ANY))
        args.append(before)
        aliases = {len(args): 0}
        body = kernel

        def kernel(*refs):
            body(*refs[:4 + num], *refs[5 + num:])
    return call(
        kernel, (pl.cdiv(rows, tile),), in_specs, w_spec,
        jax.ShapeDtypeStruct(weight.shape, F32), idx, args,
        2 * BS * BS * num * rows, num * BS * rows * 2, scratch=[pltpu.VMEM((BS, tile), BF16)], aliases=aliases,
    )


def unpack_kernel(n_direct, idx_ref, *refs):
    out_ref = refs[-1]
    step = pl.program_id(0)
    core, x_pos, y_pos = idx_ref[CORE], idx_ref[XPOS], idx_ref[YPOS]
    rows = BS // 4

    def place(mirror):
        for side in range(2):
            src = jnp.bitwise_xor(core, side)
            line = pl.ds(pl.multiple_of(src * BS, BS), BS)
            for k in range(4):
                off = jnp.bitwise_xor(x_pos, k // 2) * (2 * rows) + jnp.bitwise_xor(y_pos, k % 2) * rows
                for h in range(2):
                    spot = pl.ds(pl.multiple_of(jnp.bitwise_xor(src, h) * BS + off, rows), rows)
                    if mirror:
                        out_ref[line, spot] = refs[4 * side + k][h].T
                    else:
                        out_ref[spot, line] = refs[4 * side + k][h]

    @pl.when(step < n_direct)
    def _():
        place(False)

    @pl.when(step >= n_direct)
    def _():
        place(True)


def unpack(idx, gram, parts, dim, q, p_lo, p_hi):
    n_direct = p_hi - p_lo
    n_mirror = min(p_hi, q) - p_lo

    def in_map(t, s):
        return jnp.where(t < n_direct, t, t - n_direct), 0, 0

    def out_map(t, s):
        direct = t < n_direct
        return jnp.where(direct, p_lo + t, q), jnp.where(direct, q, p_lo + t - n_direct)

    in_specs = [pl.BlockSpec((2, BS // 4, BS), in_map) for _ in parts]
    args = list(parts)
    kernel = functools.partial(unpack_kernel, n_direct)
    aliases = None
    if gram is not None:
        in_specs.append(pl.BlockSpec(memory_space=pl.ANY))
        args.append(gram)
        aliases = {len(args): 0}
        body = kernel

        def kernel(*refs):
            body(*refs[:9], refs[-1])
    size = (n_direct + n_mirror) * 4 * BS * BS
    return call(
        kernel, (n_direct + n_mirror,), in_specs, pl.BlockSpec((2 * BS, 2 * BS), out_map),
        jax.ShapeDtypeStruct((dim, dim), BF16), idx, args, size * 64, size * 4, aliases=aliases,
    )


def solution(mesh):
    n_y = mesh.shape['fsdp']
    n_tp = mesh.shape['tp']
    mat_spec = P('stage', 'fsdp', 'tp')
    scalar_spec = P()
    pair_c = [(t, t ^ 1) for t in range(n_tp)]
    pair_x = [(t, t ^ 2) for t in range(n_tp)]
    pair_y = [(t, t ^ 1) for t in range(n_y)]

    def local_step(weight, momentum, gradient, learn_rate, mom_coef, weight_decay):
        row_dim = weight.shape[1] * n_y
        dim = weight.shape[2] * n_tp
        n_chunks = dim // (2 * BS)
        units = [(q, 0, q + 1) for q in range(n_chunks - 1)] + [(n_chunks - 1, 0, n_chunks // 2), (n_chunks - 1, n_chunks // 2, n_chunks)]
        tp = lax.axis_index('tp')
        y_pos = lax.axis_index('fsdp')
        core = lax.rem(tp, 2)
        x_pos = tp // 2
        table = []
        for q in range(n_chunks):
            table += [2 * q + core, 2 * q + 1 - core]
        table += [core, jnp.zeros_like(core), x_pos, y_pos, 2 * x_pos + y_pos, 2 * x_pos + 1 - y_pos]
        table += [2 * tp, 2 * tp + 1, 2 * tp + core, 2 * tp + 1 - core]
        order = Order(jnp.stack(table).astype(jnp.int32))

        def pair_sum(value):
            for axis, pairs in (('tp', pair_c), ('tp', pair_x), ('fsdp', pair_y)):
                value = value + lax.ppermute(value, axis, pairs)
            return value

        grad_full = gradient[0].astype(F32)
        nesterov = grad_full + mom_coef * (mom_coef * momentum[0] + grad_full)
        norm_val = jnp.sqrt(pair_sum(jnp.sum(nesterov * nesterov).reshape(1)))
        x_own = start_x(momentum[0], gradient[0], jnp.stack([mom_coef, norm_val[0] + NORM_EPS]))
        mom_old, grad_old, x_own = lax.optimization_barrier((momentum[0], gradient[0], x_own))
        mom_new = mom_coef * mom_old + grad_old.astype(F32)
        x_all = lax.all_gather(x_own, 'tp', axis=0, tiled=True)
        x_all = x_all.reshape(dim // BS, BS, x_all.shape[-1])
        pieces = [(x_all, at) for at in range(2 * n_chunks)]

        class Unit:
            def __init__(self, pieces, num):
                self.where = units[num]
                self.keep, send = gram_unit(order.idx, pieces, *self.where)
                order.after(self.keep)
                self.got = lax.ppermute(send, 'fsdp', pair_y)

            def reduce(self, wait=True):
                mine = (self.keep + self.got).astype(BF16)
                self.parts = [mine, lax.ppermute(mine, 'fsdp', pair_y), lax.ppermute(mine, 'tp', pair_x)]
                if wait:
                    order.after(mine)

            def spread(self, wait=True):
                self.parts.append(lax.ppermute(self.parts[1], 'tp', pair_x))
                self.parts += [lax.ppermute(part, 'tp', pair_c) for part in self.parts]
                if wait:
                    order.after(self.parts[1], self.parts[2])

            def place(self, gram):
                gram = unpack(order.idx, gram, self.parts, dim, *self.where)
                return gram

        last = n_chunks - 1
        flying = []
        for num in range(len(units)):
            flying.append(Unit(pieces, num))
            if num >= 2:
                flying[num - 2].reduce()
        for num in range(len(units)):
            if num > last - 1:
                flying[num].reduce(wait=False)
            flying[num].spread(wait=False)
        gram = None
        for unit in flying:
            gram = unit.place(gram)
        for _ in range(NS_STEPS - 1):
            flying, new_pieces = [], []
            poly = poly_rows(order.idx, gram, 0)
            for q in range(n_chunks):
                order.after(poly)
                mine = update_chunk(order.idx, poly, pieces, q)
                order.after(mine)
                new_pieces += [(mine, ZERO), (lax.ppermute(mine, 'tp', pair_c), ZERO)]
                if q >= 1 and q < last:
                    flying[q - 1].reduce()
                if q < last:
                    poly = poly_rows(order.idx, gram, 2 * (q + 1))
                    order.after(poly)
                    if q >= 1:
                        flying[q - 1].spread()
                    flying.append(Unit(new_pieces, q))
            flying.append(Unit(new_pieces, last))
            flying[last - 1].reduce()
            flying.append(Unit(new_pieces, last + 1))
            flying[last - 1].spread(wait=False)
            gram = None
            for num in range(last - 1):
                gram = flying[num].place(gram)
            for unit in flying[last:]:
                unit.reduce(wait=False)
                unit.spread(wait=False)
            for unit in flying[last - 1:]:
                gram = unit.place(gram)
            pieces = new_pieces
        step_scale = learn_rate * 0.2 * math.sqrt(row_dim)
        scalars = jnp.stack([1.0 - learn_rate * weight_decay, step_scale])
        new_weight = None
        for half in range(2):
            poly = poly_rows(order.idx, gram, MINE + half)
            new_weight = finish(order.idx, scalars, poly, weight[0], pieces, half, new_weight)
        return new_weight[None], mom_new[None]


    return jax.shard_map(local_step, mesh=mesh, in_specs=(mat_spec,) * 3 + (scalar_spec,) * 3, out_specs=(mat_spec, mat_spec), check_vma=False)
```

time: 4620 us -> 2940 us (0.64)
  waiting for transfers between devices: 3810 us -> 1110 us
  Pallas kernels: 0 us -> 1560 us
  matrix products: 690 us -> 0 us
  starting transfers between devices: 3.76 us -> 117 us
    all_gather x20 -> x1, waiting for transfers between devices: 2880 us -> 266 us  [local_step(): x_all = lax.all_gather(x_own, 'tp', axis=0, tiled=True)]
    pallas_call x0 -> x87, Pallas kernels: none -> 1560 us  [the longest x86 1540 us: call(): pl.pallas_call(kernel, grid_spec=pltpu.PrefetchScalarGridSpec(num_scalar_...]
    reduce_scatter x5 -> x0, waiting for transfers between devices: 932 us -> none  [local_step(): lax.psum_scatter(gram_part, 'fsdp', scatter_dimension=2, tiled=True)]
    ppermute x0 -> x219, waiting for transfers between devices: none -> 846 us  [the longest x25 339 us: __init__(): self.got = lax.ppermute(send, 'fsdp', pair_y)]
    dot_general x15 -> x0, matrix products: 690 us -> none  [the longest x5 292 us: local_step(): jnp.einsum('erc,erd->ecd', x_iter, x_rows, preferred_element_type=jnp.flo...]
    ppermute x0 -> x219, starting transfers between devices: none -> 117 us  [the longest x25 27.6 us: __init__(): self.got = lax.ppermute(send, 'fsdp', pair_y)]
  transfers between devices with their start and end apart: 25 -> 220, of which waited for: 25 -> 59; matrix products, arithmetic and copies ran while one was open for 0% -> 2% of each run, Pallas kernels for 0% -> 20%
where the time goes in v1:
time: 2940 us; the launch traced here: 2930 us
  Pallas kernels  1560 us (53%)
  waiting for transfers between devices  1110 us (38%)
  starting transfers between devices  117 us (4%)
  other arithmetic  75.5 us (3%)
  local copies, waits for them, and re-layouts  45.5 us (2%)
    pallas_call x86, Pallas kernels, call(): pl.pallas_call(kernel, grid_spec=pltpu.PrefetchScalarGridSpec(num_scalar_...  1540 us
    ppermute x25, waiting for transfers between devices, __init__(): self.got = lax.ppermute(send, 'fsdp', pair_y)  339 us
    ppermute x25, waiting for transfers between devices, reduce(): lax.ppermute(mine, 'fsdp', pair_y)  276 us
    all_gather x1, waiting for transfers between devices, local_step(): x_all = lax.all_gather(x_own, 'tp', axis=0, tiled=True)  266 us
    ppermute x25, waiting for transfers between devices, spread(): self.parts.append(lax.ppermute(self.parts[1], 'tp', pair_x))  162 us
    ppermute x25, waiting for transfers between devices, reduce(): lax.ppermute(mine, 'tp', pair_x)  62.4 us
  transfers between devices with their start and end apart: 220, of which 59 were waited for; matrix products, arithmetic and copies ran while one was open for 2% of the time, Pallas kernels for 20%

profile of v1, /device:TPU:0, one launch (start us, length us, event | category | flops | bytes accessed | tf_op | source)
XLA Modules:
  0.0 2926.4 jit_solution(7380459084265380706)
XLA Ops:
  54.2 265.9 %all-gather.2.cloned.1.call-done = bf16[4096,5504]{1,0:T(8,128)(2,1)} async-done(((bf16[1024,5504]{1,0:T(8,128)(2,1)}), bf16[4096,5504]{1,0:T(8,128)(2,1)}) %all-gather.2.cloned.1.call-update) | async-done | bytes 45088784 | tf_op jit(solution)/shard_map/all_gather | solution.py:301
  392.9 25.8 collective-permute-done.29.refs_2_
  446.9 31.1 %collective-permute-done.15.refs_2_ = bf16[4,128,512]{2,1,0:T(8,128)(2,1)S(1)} collective-permute-done((bf16[4,128,512]{2,1,0:T(8,128)(2,1)S(1)}, bf16[4,128,512]{2,1,0:T(8,128)(2,1)S(1)}, u32[]{:S(2)}, u32[]{:S(2)}) %collective-permute-start.15) | collective-permute-done | bytes 524320 | tf_op jit(solution)/shard_map/ppermute | solution.py:314
  497.8 26.9 collective-permute-done.17.refs_4_
  615.3 32.6 %shard_map.88.rows_ref.refs_0_.refs_2_.refs_4_.refs_6_ = bf16[1,512,5504]{2,1,0:T(8,128)(2,1)} custom-call(s32[18]{0:T(128)} %stack.84.idx_ref.refs_0_, bf16[512,4096]{1,0:T(8,128)(2,1)} %shard_map.87.b_ref, bf16[8,512,5504]{2,1,0:T(8,128)(2,1)} %bitcast.75, bf16[8,512,5504]{2,1,0:T(8,128)(2,1)} %bitcast.76, bf16[8,512,5504]{2,1,0:T(8,128)(2,1)} %bitcast.77, ...), custom_call_target="tpu_custom_call" | custom-call | flops 23085449216 | bytes 45088768 | tf_op jit(solution)/shard_map/pallas_call | solution.py:26
  647.9 24.8 shard_map.89.b_ref
  683.4 32.8 %shard_map.91.rows_ref.refs_2_.refs_6_.refs_8_ = bf16[1,512,5504]{2,1,0:T(8,128)(2,1)} custom-call(s32[18]{0:T(128)} %stack.84.idx_ref.refs_0_, bf16[512,4096]{1,0:T(8,128)(2,1)} %shard_map.89.b_ref, bf16[8,512,5504]{2,1,0:T(8,128)(2,1)} %bitcast.87, bf16[8,512,5504]{2,1,0:T(8,128)(2,1)} %bitcast.84, bf16[8,512,5504]{2,1,0:T(8,128)(2,1)} %bitcast.85, ...), custom_call_target="tpu_custom_call" | custom-call | flops 23085449216 | bytes 45088768 | tf_op jit(solution)/shard_map/pallas_call | solution.py:26
  771.9 32.6 %shard_map.94.rows_ref.refs_4_.refs_10_.refs_0_ = bf16[1,512,5504]{2,1,0:T(8,128)(2,1)} custom-call(s32[18]{0:T(128)} %stack.84.idx_ref.refs_0_, bf16[512,4096]{1,0:T(8,128)(2,1)} %shard_map.92.b_ref, bf16[8,512,5504]{2,1,0:T(8,128)(2,1)} %bitcast.91, bf16[8,512,5504]{2,1,0:T(8,128)(2,1)} %bitcast.92, bf16[8,512,5504]{2,1,0:T(8,128)(2,1)} %bitcast.93, ...), custom_call_target="tpu_custom_call" | custom-call | flops 23085449216 | bytes 45088768 | tf_op jit(solution)/shard_map/pallas_call | solution.py:26
  878.1 32.6 %shard_map.97.rows_ref.refs_2_.refs_6_ = bf16[1,512,5504]{2,1,0:T(8,128)(2,1)} custom-call(s32[18]{0:T(128)} %stack.84.idx_ref.refs_0_, bf16[512,4096]{1,0:T(8,128)(2,1)} %shard_map.95.b_ref, bf16[8,512,5504]{2,1,0:T(8,128)(2,1)} %bitcast.99, bf16[8,512,5504]{2,1,0:T(8,128)(2,1)} %bitcast.100, bf16[8,512,5504]{2,1,0:T(8,128)(2,1)} %bitcast.101, ...), custom_call_target="tpu_custom_call" | custom-call | flops 23085449216 | bytes 45088768 | tf_op jit(solution)/shard_map/pallas_call | solution.py:26
  925.5 44.7 %collective-permute-done.62 = f32[4,128,512]{2,1,0:T(8,128)S(1)} collective-permute-done((f32[4,128,512]{2,1,0:T(8,128)}, f32[4,128,512]{2,1,0:T(8,128)S(1)}, u32[]{:S(2)}, u32[]{:S(2)}) %collective-permute-start.62) | collective-permute-done | bytes 1048608 | tf_op jit(solution)/shard_map/ppermute | solution.py:310
  1015.7 36.8 %collective-permute-done.70.refs_2_ = bf16[6,128,512]{2,1,0:T(8,128)(2,1)S(1)} collective-permute-done((bf16[6,128,512]{2,1,0:T(8,128)(2,1)}, bf16[6,128,512]{2,1,0:T(8,128)(2,1)S(1)}, u32[]{:S(2)}, u32[]{:S(2)}) %collective-permute-start.70) | collective-permute-done | bytes 786464 | tf_op jit(solution)/shard_map/ppermute | solution.py:314
  1160.1 32.6 %shard_map.106.rows_ref.refs_0_.refs_2_.refs_4_.refs_6_ = bf16[1,512,5504]{2,1,0:T(8,128)(2,1)} custom-call(s32[18]{0:T(128)} %stack.84.idx_ref.refs_0_, bf16[512,4096]{1,0:T(8,128)(2,1)} %shard_map.105.b_ref, bf16[1,512,5504]{2,1,0:T(8,128)(2,1)} %shard_map.88.rows_ref.refs_0_.refs_2_.refs_4_.refs_6_, bf16[1,512,5504]{2,1,0:T(8,128)(2,1)} %copy-done.4, ...), custom_call_target="tpu_custom_call" | custom-call | flops 23085449216 | bytes 45088768 | tf_op jit(solution)/shard_map/pallas_call | solution.py:26
  1228.8 32.7 %shard_map.109.rows_ref.refs_2_.refs_6_.refs_8_ = bf16[1,512,5504]{2,1,0:T(8,128)(2,1)} custom-call(s32[18]{0:T(128)} %stack.84.idx_ref.refs_0_, bf16[512,4096]{1,0:T(8,128)(2,1)} %shard_map.107.b_ref, bf16[1,512,5504]{2,1,0:T(8,128)(2,1)} %shard_map.88.rows_ref.refs_0_.refs_2_.refs_4_.refs_6_, bf16[1,512,5504]{2,1,0:T(8,128)(2,1)} %copy-done.4, ...), custom_call_target="tpu_custom_call" | custom-call | flops 23085449216 | bytes 45088768 | tf_op jit(solution)/shard_map/pallas_call | solution.py:26
  1317.5 32.6 %shard_map.112.rows_ref.refs_4_.refs_10_.refs_0_ = bf16[1,512,5504]{2,1,0:T(8,128)(2,1)} custom-call(s32[18]{0:T(128)} %stack.84.idx_ref.refs_0_, bf16[512,4096]{1,0:T(8,128)(2,1)} %shard_map.110.b_ref, bf16[1,512,5504]{2,1,0:T(8,128)(2,1)} %shard_map.88.rows_ref.refs_0_.refs_2_.refs_4_.refs_6_, bf16[1,512,5504]{2,1,0:T(8,128)(2,1)} %copy-done.4, ...), custom_call_target="tpu_custom_call" | custom-call | flops 23085449216 | bytes 45088768 | tf_op jit(solution)/shard_map/pallas_call | solution.py:26
  1423.7 32.6 %shard_map.115.rows_ref.refs_2_.refs_6_ = bf16[1,512,5504]{2,1,0:T(8,128)(2,1)} custom-call(s32[18]{0:T(128)} %stack.84.idx_ref.refs_0_, bf16[512,4096]{1,0:T(8,128)(2,1)} %shard_map.113.b_ref, bf16[1,512,5504]{2,1,0:T(8,128)(2,1)} %shard_map.88.rows_ref.refs_0_.refs_2_.refs_4_.refs_6_, bf16[1,512,5504]{2,1,0:T(8,128)(2,1)} %copy-done.4, ...), custom_call_target="tpu_custom_call" | custom-call | flops 23085449216 | bytes 45088768 | tf_op jit(solution)/shard_map/pallas_call | solution.py:26
  1471.0 44.9 %collective-permute-done.106 = f32[4,128,512]{2,1,0:T(8,128)S(1)} collective-permute-done((f32[4,128,512]{2,1,0:T(8,128)}, f32[4,128,512]{2,1,0:T(8,128)S(1)}, u32[]{:S(2)}, u32[]{:S(2)}) %collective-permute-start.106) | collective-permute-done | bytes 1048608 | tf_op jit(solution)/shard_map/ppermute | solution.py:310
  1561.6 36.8 %collective-permute-done.114.refs_2_ = bf16[6,128,512]{2,1,0:T(8,128)(2,1)S(1)} collective-permute-done((bf16[6,128,512]{2,1,0:T(8,128)(2,1)}, bf16[6,128,512]{2,1,0:T(8,128)(2,1)S(1)}, u32[]{:S(2)}, u32[]{:S(2)}) %collective-permute-start.114) | collective-permute-done | bytes 786464 | tf_op jit(solution)/shard_map/ppermute | solution.py:314
  1706.0 32.6 %shard_map.124.rows_ref.refs_0_.refs_2_.refs_4_.refs_6_ = bf16[1,512,5504]{2,1,0:T(8,128)(2,1)} custom-call(s32[18]{0:T(128)} %stack.84.idx_ref.refs_0_, bf16[512,4096]{1,0:T(8,128)(2,1)} %shard_map.123.b_ref, bf16[1,512,5504]{2,1,0:T(8,128)(2,1)} %shard_map.106.rows_ref.refs_0_.refs_2_.refs_4_.refs_6_, bf16[1,512,5504]{2,1,0:T(8,128)(2,1)} %copy-done.2, ...), custom_call_target="tpu_custom_call" | custom-call | flops 23085449216 | bytes 45088768 | tf_op jit(solution)/shard_map/pallas_call | solution.py:26
  1774.7 32.7 %shard_map.127.rows_ref.refs_2_.refs_6_.refs_8_ = bf16[1,512,5504]{2,1,0:T(8,128)(2,1)} custom-call(s32[18]{0:T(128)} %stack.84.idx_ref.refs_0_, bf16[512,4096]{1,0:T(8,128)(2,1)} %shard_map.125.b_ref, bf16[1,512,5504]{2,1,0:T(8,128)(2,1)} %shard_map.106.rows_ref.refs_0_.refs_2_.refs_4_.refs_6_, bf16[1,512,5504]{2,1,0:T(8,128)(2,1)} %copy-done.2, ...), custom_call_target="tpu_custom_call" | custom-call | flops 23085449216 | bytes 45088768 | tf_op jit(solution)/shard_map/pallas_call | solution.py:26
  1863.2 32.6 %shard_map.130.rows_ref.refs_4_.refs_10_.refs_0_ = bf16[1,512,5504]{2,1,0:T(8,128)(2,1)} custom-call(s32[18]{0:T(128)} %stack.84.idx_ref.refs_0_, bf16[512,4096]{1,0:T(8,128)(2,1)} %shard_map.128.b_ref, bf16[1,512,5504]{2,1,0:T(8,128)(2,1)} %shard_map.106.rows_ref.refs_0_.refs_2_.refs_4_.refs_6_, bf16[1,512,5504]{2,1,0:T(8,128)(2,1)} %copy-done.2, ...), custom_call_target="tpu_custom_call" | custom-call | flops 23085449216 | bytes 45088768 | tf_op jit(solution)/shard_map/pallas_call | solution.py:26
  1969.6 32.5 %shard_map.133.rows_ref.refs_2_.refs_6_ = bf16[1,512,5504]{2,1,0:T(8,128)(2,1)} custom-call(s32[18]{0:T(128)} %stack.84.idx_ref.refs_0_, bf16[512,4096]{1,0:T(8,128)(2,1)} %shard_map.131.b_ref, bf16[1,512,5504]{2,1,0:T(8,128)(2,1)} %shard_map.106.rows_ref.refs_0_.refs_2_.refs_4_.refs_6_, bf16[1,512,5504]{2,1,0:T(8,128)(2,1)} %copy-done.2, ...), custom_call_target="tpu_custom_call" | custom-call | flops 23085449216 | bytes 45088768 | tf_op jit(solution)/shard_map/pallas_call | solution.py:26
  2017.0 44.6 %collective-permute-done.150 = f32[4,128,512]{2,1,0:T(8,128)S(1)} collective-permute-done((f32[4,128,512]{2,1,0:T(8,128)}, f32[4,128,512]{2,1,0:T(8,128)S(1)}, u32[]{:S(2)}, u32[]{:S(2)}) %collective-permute-start.150) | collective-permute-done | bytes 1048608 | tf_op jit(solution)/shard_map/ppermute | solution.py:310
  2107.4 36.8 %collective-permute-done.158.refs_2_ = bf16[6,128,512]{2,1,0:T(8,128)(2,1)S(1)} collective-permute-done((bf16[6,128,512]{2,1,0:T(8,128)(2,1)}, bf16[6,128,512]{2,1,0:T(8,128)(2,1)S(1)}, u32[]{:S(2)}, u32[]{:S(2)}) %collective-permute-start.158) | collective-permute-done | bytes 786464 | tf_op jit(solution)/shard_map/ppermute | solution.py:314
  2251.8 32.6 %shard_map.142.rows_ref.refs_0_.refs_2_.refs_4_.refs_6_ = bf16[1,512,5504]{2,1,0:T(8,128)(2,1)} custom-call(s32[18]{0:T(128)} %stack.84.idx_ref.refs_0_, bf16[512,4096]{1,0:T(8,128)(2,1)} %shard_map.141.b_ref, bf16[1,512,5504]{2,1,0:T(8,128)(2,1)} %shard_map.124.rows_ref.refs_0_.refs_2_.refs_4_.refs_6_, bf16[1,512,5504]{2,1,0:T(8,128)(2,1)} %copy-done.3, ...), custom_call_target="tpu_custom_call" | custom-call | flops 23085449216 | bytes 45088768 | tf_op jit(solution)/shard_map/pallas_call | solution.py:26
  2320.4 32.7 %shard_map.145.rows_ref.refs_2_.refs_6_.refs_8_ = bf16[1,512,5504]{2,1,0:T(8,128)(2,1)} custom-call(s32[18]{0:T(128)} %stack.84.idx_ref.refs_0_, bf16[512,4096]{1,0:T(8,128)(2,1)} %shard_map.143.b_ref, bf16[1,512,5504]{2,1,0:T(8,128)(2,1)} %shard_map.124.rows_ref.refs_0_.refs_2_.refs_4_.refs_6_, bf16[1,512,5504]{2,1,0:T(8,128)(2,1)} %copy-done.3, ...), custom_call_target="tpu_custom_call" | custom-call | flops 23085449216 | bytes 45088768 | tf_op jit(solution)/shard_map/pallas_call | solution.py:26
  2370.0 24.7 shard_map.146.b_ref
  2409.2 32.6 %shard_map.148.rows_ref.refs_4_.refs_10_.refs_0_.refs_8_ = bf16[1,512,5504]{2,1,0:T(8,128)(2,1)} custom-call(s32[18]{0:T(128)} %stack.84.idx_ref.refs_0_, bf16[512,4096]{1,0:T(8,128)(2,1)} %shard_map.146.b_ref, bf16[1,512,5504]{2,1,0:T(8,128)(2,1)} %shard_map.124.rows_ref.refs_0_.refs_2_.refs_4_.refs_6_, bf16[1,512,5504]{2,1,0:T(8,128)(2,1)} %copy-done.3, ...), custom_call_target="tpu_custom_call" | custom-call | flops 23085449216 | bytes 45088768 | tf_op jit(solution)/shard_map/pallas_call | solution.py:26
  2515.4 32.6 %shard_map.151.rows_ref.refs_2_.refs_6_.refs_10_ = bf16[1,512,5504]{2,1,0:T(8,128)(2,1)} custom-call(s32[18]{0:T(128)} %stack.84.idx_ref.refs_0_, bf16[512,4096]{1,0:T(8,128)(2,1)} %shard_map.149.b_ref, bf16[1,512,5504]{2,1,0:T(8,128)(2,1)} %shard_map.124.rows_ref.refs_0_.refs_2_.refs_4_.refs_6_, bf16[1,512,5504]{2,1,0:T(8,128)(2,1)} %copy-done.3, ...), custom_call_target="tpu_custom_call" | custom-call | flops 23085449216 | bytes 45088768 | tf_op jit(solution)/shard_map/pallas_call | solution.py:26
  2562.7 44.8 %collective-permute-done.194 = f32[4,128,512]{2,1,0:T(8,128)S(1)} collective-permute-done((f32[4,128,512]{2,1,0:T(8,128)}, f32[4,128,512]{2,1,0:T(8,128)S(1)}, u32[]{:S(2)}, u32[]{:S(2)}) %collective-permute-start.194) | collective-permute-done | bytes 1048608 | tf_op jit(solution)/shard_map/ppermute | solution.py:310
  2653.2 36.8 %collective-permute-done.202.refs_2_ = bf16[6,128,512]{2,1,0:T(8,128)(2,1)S(1)} collective-permute-done((bf16[6,128,512]{2,1,0:T(8,128)(2,1)}, bf16[6,128,512]{2,1,0:T(8,128)(2,1)S(1)}, u32[]{:S(2)}, u32[]{:S(2)}) %collective-permute-start.202) | collective-permute-done | bytes 786464 | tf_op jit(solution)/shard_map/ppermute | solution.py:314
  2845.0 37.3 %shard_map.161.refs_12_ = f32[5504,1024]{1,0:T(8,128)} custom-call(s32[18]{0:T(128)} %stack.84.idx_ref.refs_0_, f32[2]{0:T(128)} %pad_maximum_fusion.1.scal_ref.refs_1_, bf16[512,4096]{1,0:T(8,128)(2,1)} %shard_map.160.b_ref, f32[5504,1024]{1,0:T(8,128)} %bitcast.111, bf16[1,512,5504]{2,1,0:T(8,128)(2,1)} %shard_map.142.rows_ref.refs_0_.refs_2_.refs_4_.refs_6_, ...), custom_call_target="tpu_custom_call" | custom-call | flops 23085449216 | bytes 45088768 | tf_op jit(solution)/shard_map/pallas_call | solution.py:26
  2882.3 37.1 %shard_map.162 = f32[5504,1024]{1,0:T(8,128)} custom-call(s32[18]{0:T(128)} %stack.84.idx_ref.refs_0_, f32[2]{0:T(128)} %pad_maximum_fusion.1.scal_ref.refs_1_, bf16[512,4096]{1,0:T(8,128)(2,1)} %shard_map.159.refs_2_, f32[5504,1024]{1,0:T(8,128)} %bitcast.112, ...), custom_call_target="tpu_custom_call", output_to_operand_aliasing={{}: (12, {})} | custom-call | flops 23085449216 | bytes 45088768 | tf_op jit(solution)/shard_map/pallas_call | solution.py:26
  (782 shorter events, 1583.9 us)
Async XLA Ops:
  7.2 313.0 %all-gather.2.cloned.1.call-start = ((), (), s32[]{:S(2)}) async-start(), calls=%async_computation | async-start | bytes 56360960 | tf_op jit(solution)/shard_map/all_gather | solution.py:301
  361.7 78.8 %collective-permute-start.5 = (f32[6,128,512]{2,1,0:T(8,128)}, f32[6,128,512]{2,1,0:T(8,128)}, u32[]{:S(2)}, u32[]{:S(2)}) collective-permute-start(f32[6,128,512]{2,1,0:T(8,128)} %get-tuple-element.162), channel_id=1, source_target_pairs={{0,4},{4,0},{1,5},{5,1},{2,6},{6,2},{3,7},{7,3}} | collective-permute-start | bytes 4718600 | tf_op jit(solution)/shard_map/ppermute | solution.py:310
  440.5 54.6 %collective-permute-start.6 = (f32[4,128,512]{2,1,0:T(8,128)}, f32[4,128,512]{2,1,0:T(8,128)S(1)}, u32[]{:S(2)}, u32[]{:S(2)}) collective-permute-start(f32[4,128,512]{2,1,0:T(8,128)} %get-tuple-element.164), channel_id=1, source_target_pairs={{0,4},{4,0},{1,5},{5,1},{2,6},{6,2},{3,7},{7,3}} | collective-permute-start | bytes 3145736 | tf_op jit(solution)/shard_map/ppermute | solution.py:310
  804.5 54.7 %collective-permute-start.51 = (bf16[1,512,5504]{2,1,0:T(8,128)(2,1)}, bf16[1,512,5504]{2,1,0:T(8,128)(2,1)S(1)}, u32[]{:S(2)}, u32[]{:S(2)}) collective-permute-start(bf16[1,512,5504]{2,1,0:T(8,128)(2,1)} %shard_map.94.rows_ref.refs_4_.refs_10_.refs_0_), channel_id=1, source_target_pairs={{0,1},{1,0},{2,3},{3,2},{4,5},{5,4},{6,7},{7,6}} | collective-permute-start | bytes 16908296 | tf_op jit(solution)/shard_map/ppermute | solution.py:348
  910.7 73.3 %collective-permute-start.53 = (bf16[1,512,5504]{2,1,0:T(8,128)(2,1)}, bf16[1,512,5504]{2,1,0:T(8,128)(2,1)S(1)}, u32[]{:S(2)}, u32[]{:S(2)}) collective-permute-start(bf16[1,512,5504]{2,1,0:T(8,128)(2,1)} %shard_map.97.rows_ref.refs_2_.refs_6_), channel_id=1, source_target_pairs={{0,1},{1,0},{2,3},{3,2},{4,5},{5,4},{6,7},{7,6}} | collective-permute-start | bytes 16908296 | tf_op jit(solution)/shard_map/ppermute | solution.py:348
  910.7 62.5 %collective-permute-start.52 = (f32[6,128,512]{2,1,0:T(8,128)}, f32[6,128,512]{2,1,0:T(8,128)}, u32[]{:S(2)}, u32[]{:S(2)}) collective-permute-start(f32[6,128,512]{2,1,0:T(8,128)} %get-tuple-element.191), channel_id=1, source_target_pairs={{0,4},{4,0},{1,5},{5,1},{2,6},{6,2},{3,7},{7,3}} | collective-permute-start | bytes 4718600 | tf_op jit(solution)/shard_map/ppermute | solution.py:310
  924.7 52.1 %collective-permute-start.82 = (bf16[2,128,512]{2,1,0:T(8,128)(2,1)}, bf16[2,128,512]{2,1,0:T(8,128)(2,1)}, u32[]{:S(2)}, u32[]{:S(2)}) collective-permute-start(bf16[2,128,512]{2,1,0:T(8,128)(2,1)} %copy-done.109), channel_id=1, source_target_pairs={{0,2},{1,3},{2,0},{3,1},{4,6},{5,7},{6,4},{7,5}} | collective-permute-start | bytes 786440 | tf_op jit(solution)/shard_map/ppermute | solution.py:319
  999.3 54.8 %collective-permute-start.54 = (f32[4,128,512]{2,1,0:T(8,128)}, f32[4,128,512]{2,1,0:T(8,128)S(1)}, u32[]{:S(2)}, u32[]{:S(2)}) collective-permute-start(f32[4,128,512]{2,1,0:T(8,128)} %get-tuple-element.195), channel_id=1, source_target_pairs={{0,4},{4,0},{1,5},{5,1},{2,6},{6,2},{3,7},{7,3}} | collective-permute-start | bytes 3145736 | tf_op jit(solution)/shard_map/ppermute | solution.py:310
  1073.7 54.2 %collective-permute-start.58 = (bf16[4,128,512]{2,1,0:T(8,128)(2,1)S(1)}, bf16[4,128,512]{2,1,0:T(8,128)(2,1)}, u32[]{:S(2)}, u32[]{:S(2)}) collective-permute-start(bf16[4,128,512]{2,1,0:T(8,128)(2,1)S(1)} %add_convert_fusion.15.refs_1_), channel_id=1, source_target_pairs={{0,1},{1,0},{2,3},{3,2},{4,5},{5,4},{6,7},{7,6}} | collective-permute-start | bytes 1572872 | tf_op jit(solution)/shard_map/ppermute | solution.py:320
  1074.2 53.7 %collective-permute-start.59 = (bf16[4,128,512]{2,1,0:T(8,128)(2,1)}, bf16[4,128,512]{2,1,0:T(8,128)(2,1)}, u32[]{:S(2)}, u32[]{:S(2)}) collective-permute-start(bf16[4,128,512]{2,1,0:T(8,128)(2,1)} %collective-permute-done.55.refs_2_), channel_id=1, source_target_pairs={{0,1},{1,0},{2,3},{3,2},{4,5},{5,4},{6,7},{7,6}} | collective-permute-start | bytes 1572872 | tf_op jit(solution)/shard_map/ppermute | solution.py:320
  1350.1 54.8 %collective-permute-start.95 = (bf16[1,512,5504]{2,1,0:T(8,128)(2,1)}, bf16[1,512,5504]{2,1,0:T(8,128)(2,1)S(1)}, u32[]{:S(2)}, u32[]{:S(2)}) collective-permute-start(bf16[1,512,5504]{2,1,0:T(8,128)(2,1)} %shard_map.112.rows_ref.refs_4_.refs_10_.refs_0_), channel_id=1, source_target_pairs={{0,1},{1,0},{2,3},{3,2},{4,5},{5,4},{6,7},{7,6}} | collective-permute-start | bytes 16908296 | tf_op jit(solution)/shard_map/ppermute | solution.py:348
  1456.3 73.3 %collective-permute-start.97 = (bf16[1,512,5504]{2,1,0:T(8,128)(2,1)}, bf16[1,512,5504]{2,1,0:T(8,128)(2,1)S(1)}, u32[]{:S(2)}, u32[]{:S(2)}) collective-permute-start(bf16[1,512,5504]{2,1,0:T(8,128)(2,1)} %shard_map.115.rows_ref.refs_2_.refs_6_), channel_id=1, source_target_pairs={{0,1},{1,0},{2,3},{3,2},{4,5},{5,4},{6,7},{7,6}} | collective-permute-start | bytes 16908296 | tf_op jit(solution)/shard_map/ppermute | solution.py:348
  1456.3 62.3 %collective-permute-start.96 = (f32[6,128,512]{2,1,0:T(8,128)}, f32[6,128,512]{2,1,0:T(8,128)}, u32[]{:S(2)}, u32[]{:S(2)}) collective-permute-start(f32[6,128,512]{2,1,0:T(8,128)} %get-tuple-element.222), channel_id=1, source_target_pairs={{0,4},{4,0},{1,5},{5,1},{2,6},{6,2},{3,7},{7,3}} | collective-permute-start | bytes 4718600 | tf_op jit(solution)/shard_map/ppermute | solution.py:310
  1545.2 54.8 %collective-permute-start.98 = (f32[4,128,512]{2,1,0:T(8,128)}, f32[4,128,512]{2,1,0:T(8,128)S(1)}, u32[]{:S(2)}, u32[]{:S(2)}) collective-permute-start(f32[4,128,512]{2,1,0:T(8,128)} %get-tuple-element.226), channel_id=1, source_target_pairs={{0,4},{4,0},{1,5},{5,1},{2,6},{6,2},{3,7},{7,3}} | collective-permute-start | bytes 3145736 | tf_op jit(solution)/shard_map/ppermute | solution.py:310
  1619.6 54.2 %collective-permute-start.102 = (bf16[4,128,512]{2,1,0:T(8,128)(2,1)S(1)}, bf16[4,128,512]{2,1,0:T(8,128)(2,1)}, u32[]{:S(2)}, u32[]{:S(2)}) collective-permute-start(bf16[4,128,512]{2,1,0:T(8,128)(2,1)S(1)} %add_convert_fusion.12.refs_1_), channel_id=1, source_target_pairs={{0,1},{1,0},{2,3},{3,2},{4,5},{5,4},{6,7},{7,6}} | collective-permute-start | bytes 1572872 | tf_op jit(solution)/shard_map/ppermute | solution.py:320
  1620.1 53.7 %collective-permute-start.103 = (bf16[4,128,512]{2,1,0:T(8,128)(2,1)}, bf16[4,128,512]{2,1,0:T(8,128)(2,1)}, u32[]{:S(2)}, u32[]{:S(2)}) collective-permute-start(bf16[4,128,512]{2,1,0:T(8,128)(2,1)} %collective-permute-done.99.refs_2_), channel_id=1, source_target_pairs={{0,1},{1,0},{2,3},{3,2},{4,5},{5,4},{6,7},{7,6}} | collective-permute-start | bytes 1572872 | tf_op jit(solution)/shard_map/ppermute | solution.py:320
  1895.7 54.8 %collective-permute-start.139 = (bf16[1,512,5504]{2,1,0:T(8,128)(2,1)}, bf16[1,512,5504]{2,1,0:T(8,128)(2,1)S(1)}, u32[]{:S(2)}, u32[]{:S(2)}) collective-permute-start(bf16[1,512,5504]{2,1,0:T(8,128)(2,1)} %shard_map.130.rows_ref.refs_4_.refs_10_.refs_0_), channel_id=1, source_target_pairs={{0,1},{1,0},{2,3},{3,2},{4,5},{5,4},{6,7},{7,6}} | collective-permute-start | bytes 16908296 | tf_op jit(solution)/shard_map/ppermute | solution.py:348
  2002.1 73.3 %collective-permute-start.141 = (bf16[1,512,5504]{2,1,0:T(8,128)(2,1)}, bf16[1,512,5504]{2,1,0:T(8,128)(2,1)S(1)}, u32[]{:S(2)}, u32[]{:S(2)}) collective-permute-start(bf16[1,512,5504]{2,1,0:T(8,128)(2,1)} %shard_map.133.rows_ref.refs_2_.refs_6_), channel_id=1, source_target_pairs={{0,1},{1,0},{2,3},{3,2},{4,5},{5,4},{6,7},{7,6}} | collective-permute-start | bytes 16908296 | tf_op jit(solution)/shard_map/ppermute | solution.py:348
  2002.1 62.4 %collective-permute-start.140 = (f32[6,128,512]{2,1,0:T(8,128)}, f32[6,128,512]{2,1,0:T(8,128)}, u32[]{:S(2)}, u32[]{:S(2)}) collective-permute-start(f32[6,128,512]{2,1,0:T(8,128)} %get-tuple-element.253), channel_id=1, source_target_pairs={{0,4},{4,0},{1,5},{5,1},{2,6},{6,2},{3,7},{7,3}} | collective-permute-start | bytes 4718600 | tf_op jit(solution)/shard_map/ppermute | solution.py:310
  2016.0 52.1 %collective-permute-start.170 = (bf16[2,128,512]{2,1,0:T(8,128)(2,1)}, bf16[2,128,512]{2,1,0:T(8,128)(2,1)}, u32[]{:S(2)}, u32[]{:S(2)}) collective-permute-start(bf16[2,128,512]{2,1,0:T(8,128)(2,1)} %copy-done.108), channel_id=1, source_target_pairs={{0,2},{1,3},{2,0},{3,1},{4,6},{5,7},{6,4},{7,5}} | collective-permute-start | bytes 786440 | tf_op jit(solution)/shard_map/ppermute | solution.py:319
  2090.9 54.9 %collective-permute-start.142 = (f32[4,128,512]{2,1,0:T(8,128)}, f32[4,128,512]{2,1,0:T(8,128)S(1)}, u32[]{:S(2)}, u32[]{:S(2)}) collective-permute-start(f32[4,128,512]{2,1,0:T(8,128)} %get-tuple-element.257), channel_id=1, source_target_pairs={{0,4},{4,0},{1,5},{5,1},{2,6},{6,2},{3,7},{7,3}} | collective-permute-start | bytes 3145736 | tf_op jit(solution)/shard_map/ppermute | solution.py:310
  2165.4 54.2 %collective-permute-start.146 = (bf16[4,128,512]{2,1,0:T(8,128)(2,1)S(1)}, bf16[4,128,512]{2,1,0:T(8,128)(2,1)}, u32[]{:S(2)}, u32[]{:S(2)}) collective-permute-start(bf16[4,128,512]{2,1,0:T(8,128)(2,1)S(1)} %add_convert_fusion.9.refs_1_), channel_id=1, source_target_pairs={{0,1},{1,0},{2,3},{3,2},{4,5},{5,4},{6,7},{7,6}} | collective-permute-start | bytes 1572872 | tf_op jit(solution)/shard_map/ppermute | solution.py:320
  2165.9 53.7 %collective-permute-start.147 = (bf16[4,128,512]{2,1,0:T(8,128)(2,1)}, bf16[4,128,512]{2,1,0:T(8,128)(2,1)}, u32[]{:S(2)}, u32[]{:S(2)}) collective-permute-start(bf16[4,128,512]{2,1,0:T(8,128)(2,1)} %collective-permute-done.143.refs_2_), channel_id=1, source_target_pairs={{0,1},{1,0},{2,3},{3,2},{4,5},{5,4},{6,7},{7,6}} | collective-permute-start | bytes 1572872 | tf_op jit(solution)/shard_map/ppermute | solution.py:320
  2441.8 54.7 %collective-permute-start.183 = (bf16[1,512,5504]{2,1,0:T(8,128)(2,1)}, bf16[1,512,5504]{2,1,0:T(8,128)(2,1)S(1)}, u32[]{:S(2)}, u32[]{:S(2)}) collective-permute-start(bf16[1,512,5504]{2,1,0:T(8,128)(2,1)} %shard_map.148.rows_ref.refs_4_.refs_10_.refs_0_.refs_8_), channel_id=1, source_target_pairs={{0,1},{1,0},{2,3},{3,2},{4,5},{5,4},{6,7},{7,6}} | collective-permute-start | bytes 16908296 | tf_op jit(solution)/shard_map/ppermute | solution.py:348
  2548.0 73.3 %collective-permute-start.185 = (bf16[1,512,5504]{2,1,0:T(8,128)(2,1)}, bf16[1,512,5504]{2,1,0:T(8,128)(2,1)S(1)}, u32[]{:S(2)}, u32[]{:S(2)}) collective-permute-start(bf16[1,512,5504]{2,1,0:T(8,128)(2,1)} %shard_map.151.rows_ref.refs_2_.refs_6_.refs_10_), channel_id=1, source_target_pairs={{0,1},{1,0},{2,3},{3,2},{4,5},{5,4},{6,7},{7,6}} | collective-permute-start | bytes 16908296 | tf_op jit(solution)/shard_map/ppermute | solution.py:348
  2548.0 62.4 %collective-permute-start.184 = (f32[6,128,512]{2,1,0:T(8,128)}, f32[6,128,512]{2,1,0:T(8,128)}, u32[]{:S(2)}, u32[]{:S(2)}) collective-permute-start(f32[6,128,512]{2,1,0:T(8,128)} %get-tuple-element.284), channel_id=1, source_target_pairs={{0,4},{4,0},{1,5},{5,1},{2,6},{6,2},{3,7},{7,3}} | collective-permute-start | bytes 4718600 | tf_op jit(solution)/shard_map/ppermute | solution.py:310
  2561.9 52.1 %collective-permute-start.214 = (bf16[2,128,512]{2,1,0:T(8,128)(2,1)}, bf16[2,128,512]{2,1,0:T(8,128)(2,1)}, u32[]{:S(2)}, u32[]{:S(2)}) collective-permute-start(bf16[2,128,512]{2,1,0:T(8,128)(2,1)} %copy-done.106), channel_id=1, source_target_pairs={{0,2},{1,3},{2,0},{3,1},{4,6},{5,7},{6,4},{7,5}} | collective-permute-start | bytes 786440 | tf_op jit(solution)/shard_map/ppermute | solution.py:319
  2636.8 54.8 %collective-permute-start.186 = (f32[4,128,512]{2,1,0:T(8,128)}, f32[4,128,512]{2,1,0:T(8,128)S(1)}, u32[]{:S(2)}, u32[]{:S(2)}) collective-permute-start(f32[4,128,512]{2,1,0:T(8,128)} %get-tuple-element.288), channel_id=1, source_target_pairs={{0,4},{4,0},{1,5},{5,1},{2,6},{6,2},{3,7},{7,3}} | collective-permute-start | bytes 3145736 | tf_op jit(solution)/shard_map/ppermute | solution.py:310
  2713.1 63.7 %collective-permute-start.201 = (bf16[4,128,512]{2,1,0:T(8,128)(2,1)}, bf16[4,128,512]{2,1,0:T(8,128)(2,1)S(1)}, u32[]{:S(2)}, u32[]{:S(2)}) collective-permute-start(bf16[4,128,512]{2,1,0:T(8,128)(2,1)} %copy-done.80), channel_id=1, source_target_pairs={{0,1},{1,0},{2,3},{3,2},{4,5},{5,4},{6,7},{7,6}} | collective-permute-start | bytes 1572872 | tf_op jit(solution)/shard_map/ppermute | solution.py:320
  2713.2 72.9 %collective-permute-start.190 = (bf16[4,128,512]{2,1,0:T(8,128)(2,1)S(1)}, bf16[4,128,512]{2,1,0:T(8,128)(2,1)S(1)}, u32[]{:S(2)}, u32[]{:S(2)}) collective-permute-start(bf16[4,128,512]{2,1,0:T(8,128)(2,1)S(1)} %add_convert_fusion.6.refs_1_), channel_id=1, source_target_pairs={{0,1},{1,0},{2,3},{3,2},{4,5},{5,4},{6,7},{7,6}} | collective-permute-start | bytes 1572872 | tf_op jit(solution)/shard_map/ppermute | solution.py:320
  2713.7 72.4 %collective-permute-start.191 = (bf16[4,128,512]{2,1,0:T(8,128)(2,1)}, bf16[4,128,512]{2,1,0:T(8,128)(2,1)S(1)}, u32[]{:S(2)}, u32[]{:S(2)}) collective-permute-start(bf16[4,128,512]{2,1,0:T(8,128)(2,1)} %collective-permute-done.187.refs_2_), channel_id=1, source_target_pairs={{0,1},{1,0},{2,3},{3,2},{4,5},{5,4},{6,7},{7,6}} | collective-permute-start | bytes 1572872 | tf_op jit(solution)/shard_map/ppermute | solution.py:320
  2724.0 62.1 %collective-permute-start.192 = (bf16[4,128,512]{2,1,0:T(8,128)(2,1)}, bf16[4,128,512]{2,1,0:T(8,128)(2,1)S(1)}, u32[]{:S(2)}, u32[]{:S(2)}) collective-permute-start(bf16[4,128,512]{2,1,0:T(8,128)(2,1)} %collective-permute-done.188.refs_3_), channel_id=1, source_target_pairs={{0,1},{1,0},{2,3},{3,2},{4,5},{5,4},{6,7},{7,6}} | collective-permute-start | bytes 1572872 | tf_op jit(solution)/shard_map/ppermute | solution.py:320
  (316 other events, 8676.8 us)
Sparse Core Ops, SparseCore 0:
  53.6 266.4 all-gather.1
